TPU v7x, 32 devices: a whole 2x2x4 slice. The times are simulated.
32 devices in a mesh: dp: 8 (over y, x, core), tensor: 4 (over z).
Axes of the slice: x: 2, y: 2, z: 4, core: 2. Of those that a mesh axis runs over, the one named last changes fastest.
Arguments:
- tokens: float32 [12544, 768], P(('dp', 'tensor')), may hold values from -6 to 6
- live_clips: int32 [8], P('dp'), may hold values from 1 to 2, as said below
- norm_gains: bfloat16 [3, 768], P(None, 'dp'), may hold values from 0.099609375 to 1.8984375
- qkv_time: bfloat16 [3, 768, 768], P(None, 'dp', 'tensor'), may hold values from -0.21875 to 0.21875
- out_time: bfloat16 [768, 768], P('tensor', 'dp'), may hold values from -0.625 to 0.625
- qkv_space: bfloat16 [3, 768, 768], P(None, 'dp', 'tensor'), may hold values from -0.21875 to 0.21875
- out_space: bfloat16 [768, 768], P('tensor', 'dp'), may hold values from -3.5 to 3.5
- up_weight: bfloat16 [768, 3072], P('dp', 'tensor'), may hold values from -0.21875 to 0.21875
- down_weight: bfloat16 [3072, 768], P('tensor', 'dp'), may hold values from -0.109375 to 0.109375
- cotangent: float32 [12544, 768], P(('dp', 'tensor')), may hold values from -6 to 6
Outputs:
- output: float32 [12544, 768], P(('dp', 'tensor'))
- grad_tokens: float32 [12544, 768], P(('dp', 'tensor'))
- grad_gains: float32 [3, 768], P(None, 'dp')
- grad_qkv_time: float32 [3, 768, 768], P(None, 'dp', 'tensor')
- grad_out_time: float32 [768, 768], P('tensor', 'dp')
- grad_qkv_space: float32 [3, 768, 768], P(None, 'dp', 'tensor')
- grad_out_space: float32 [768, 768], P('tensor', 'dp')
- grad_up: float32 [768, 3072], P('dp', 'tensor')
- grad_down: float32 [3072, 768], P('tensor', 'dp')
Inputs may be any that keep to these rules, and one draw needn't show every extreme that they name: `live_clips`: groups 2i and 2i+1 have equal counts; slots below a group's count are live, the others are padding; some pair of groups has all 2 slots live.
All inputs are finite; a program needn't handle non-finite values.
Results may differ from a plain program's by a relative error of at most 0.038.
Values may be sent and summed in bfloat16 or wider, within the bound.
A program may use at most 128 MiB of HBM per device.

v0:
```python
import jax
import jax.numpy as jnp
from jax import lax
from jax.sharding import PartitionSpec as P

HEAD_DIM = 64
PATCHES = 196
HALF = 4


epsilon = 1e-06


def partner(block, axis, stride):
    count = lax.axis_size(axis)
    route = []
    for low in range(count):
        high = low | 1 << stride
        if high != low and high < count:
            route += [(low, high), (high, low)]
    return lax.ppermute(block, axis, route)


def normalize(rows, scale_row):
    average = jnp.mean(rows, -1, keepdims=True)
    centred = rows - average
    spread = jnp.mean(centred * centred, -1, keepdims=True)
    return centred * lax.rsqrt(spread + epsilon) * scale_row


def norm_back(rows, scale_row, grad_normed):
    unused, pullback = jax.vjp(normalize, rows, scale_row)
    return pullback(grad_normed)


def exact_gelu(values):
    return jax.nn.gelu(values, approximate=False)


def spread_rows(local_part):
    return lax.all_gather(local_part, "tensor", axis=0, tiled=True)


def settle_rows(partial_sum):
    return lax.psum_scatter(
        partial_sum.astype(jnp.bfloat16), "tensor", scatter_dimension=0, tiled=True
    ).astype(jnp.float32)


def spread_grads(local_part):
    return lax.all_gather(local_part, "tensor", axis=0, tiled=True)


def settle_grads(partial_sum):
    return lax.psum_scatter(
        partial_sum.astype(jnp.bfloat16), "tensor", scatter_dimension=0, tiled=True
    ).astype(jnp.float32)


def project_heads(normed, weight_in):
    return jnp.einsum("gd,cde->cge", normed, weight_in, preferred_element_type=jnp.float32).astype(
        jnp.bfloat16
    )


def heads_back(normed, weight_in, grad_heads):
    grad_normed = jnp.einsum(
        "cge,cde->gd", grad_heads, weight_in, preferred_element_type=jnp.float32
    )
    grad_weight = jnp.einsum("gd,cge->cde", normed, grad_heads, preferred_element_type=jnp.float32)
    return (grad_normed, grad_weight)


def out_back(blended, weight_out, grad_local):
    grad_rows = spread_grads(grad_local.astype(jnp.bfloat16))
    grad_blended = jnp.einsum(
        "gd,ed->ge", grad_rows, weight_out, preferred_element_type=jnp.float32
    ).astype(jnp.bfloat16)
    grad_weight = jnp.einsum("ge,gd->ed", blended, grad_rows, preferred_element_type=jnp.float32)
    return (grad_blended, grad_weight)


def time_view(flat, slots):
    return flat.reshape(slots, HALF, PATCHES, -1, HEAD_DIM)


def space_view(flat):
    return flat.reshape(-1, PATCHES, flat.shape[1] // HEAD_DIM, HEAD_DIM)


def time_scores(query_part, key_part):
    return jnp.einsum(
        "sfphd,sgphd->sphfg", query_part, key_part, preferred_element_type=jnp.float32
    ) * HEAD_DIM ** (-0.5)


def space_scores(query_part, key_part):
    return jnp.einsum(
        "fphd,fqhd->fhpq", query_part, key_part, preferred_element_type=jnp.float32
    ) * HEAD_DIM ** (-0.5)


def time_key_grad(grad_scores, query_part):
    return jnp.einsum(
        "sphfg,sfphd->sgphd", grad_scores, query_part, preferred_element_type=jnp.float32
    ) * HEAD_DIM ** (-0.5)


def time_value_grad(weights_low, grad_mixed):
    return jnp.einsum(
        "sphfg,sfphd->sgphd", weights_low, grad_mixed, preferred_element_type=jnp.float32
    )


def on_device(
    tokens,
    live_clips,
    norm_gains,
    qkv_time,
    out_time,
    qkv_space,
    out_space,
    up_weight,
    down_weight,
    cotangent,
):
    score_scale = HEAD_DIM ** (-0.5)
    local_count = tokens.shape[0]
    position = lax.axis_index("tensor") * local_count + jnp.arange(local_count, dtype=jnp.int32)
    row_mask = jnp.where(position // (HALF * PATCHES) < live_clips[0], 1.0, 0.0).astype(
        jnp.float32
    )[:, None]
    fetched = (
        lax.all_gather(norm_gains, "dp", axis=1, tiled=True),
        lax.all_gather(qkv_time, "dp", axis=1, tiled=True),
        lax.all_gather(out_time, "dp", axis=1, tiled=True),
        lax.all_gather(qkv_space, "dp", axis=1, tiled=True),
        lax.all_gather(out_space, "dp", axis=1, tiled=True),
        lax.all_gather(up_weight, "dp", axis=0, tiled=True),
        lax.all_gather(down_weight, "dp", axis=1, tiled=True),
    )
    gains_all, time_in, time_out, space_in, space_out, up_full, down_full = fetched
    gain_rows = gains_all.astype(jnp.float32)
    normed_time = spread_rows(normalize(tokens, gain_rows[0]).astype(jnp.bfloat16))
    group_count = normed_time.shape[0]
    slots = group_count // (HALF * PATCHES)
    width_local = time_in.shape[2]
    time_heads = project_heads(normed_time, time_in)
    key_far, value_far = partner((time_heads[1], time_heads[2]), "dp", 0)
    query_time = time_view(time_heads[0], slots)
    key_time = time_view(time_heads[1], slots)
    value_time = time_view(time_heads[2], slots)
    key_both = jnp.concatenate([key_time, time_view(key_far, slots)], 1)
    value_both = jnp.concatenate([value_time, time_view(value_far, slots)], 1)
    scores = time_scores(query_time, key_both)
    time_totals = jax.nn.logsumexp(scores, -1)
    time_weights = jnp.exp(scores - time_totals[..., None])
    blended_time = jnp.einsum(
        "sphfg,sgphd->sfphd",
        time_weights.astype(jnp.bfloat16),
        value_both,
        preferred_element_type=jnp.float32,
    )
    blended_time = blended_time.astype(jnp.bfloat16).reshape(group_count, width_local)
    after_time = tokens + settle_rows(
        jnp.dot(blended_time, time_out, preferred_element_type=jnp.float32)
    )
    normed_space = spread_rows(normalize(after_time, gain_rows[1]).astype(jnp.bfloat16))
    space_heads = project_heads(normed_space, space_in)
    query_space = space_view(space_heads[0])
    key_space = space_view(space_heads[1])
    value_space = space_view(space_heads[2])
    scores = space_scores(query_space, key_space)
    space_totals = jax.nn.logsumexp(scores, -1)
    space_weights = jnp.exp(scores - space_totals[..., None])
    blended_space = jnp.einsum(
        "fhpq,fqhd->fphd",
        space_weights.astype(jnp.bfloat16),
        value_space,
        preferred_element_type=jnp.float32,
    )
    blended_space = blended_space.astype(jnp.bfloat16).reshape(group_count, width_local)
    after_space = after_time + settle_rows(
        jnp.dot(blended_space, space_out, preferred_element_type=jnp.float32)
    )
    normed_mlp = spread_rows(normalize(after_space, gain_rows[2]).astype(jnp.bfloat16))
    pre_act = jnp.dot(normed_mlp, up_full, preferred_element_type=jnp.float32)
    hidden = exact_gelu(pre_act).astype(jnp.bfloat16)
    after_mlp = after_space + settle_rows(
        jnp.dot(hidden, down_full, preferred_element_type=jnp.float32)
    )
    output = after_mlp * row_mask
    fetched = (
        lax.all_gather(norm_gains, "dp", axis=1, tiled=True),
        lax.all_gather(qkv_time, "dp", axis=1, tiled=True),
        lax.all_gather(out_time, "dp", axis=1, tiled=True),
        lax.all_gather(qkv_space, "dp", axis=1, tiled=True),
        lax.all_gather(out_space, "dp", axis=1, tiled=True),
        lax.all_gather(up_weight, "dp", axis=0, tiled=True),
        lax.all_gather(down_weight, "dp", axis=1, tiled=True),
    )
    gains_all, time_in, time_out, space_in, space_out, up_full, down_full = fetched
    gain_rows = gains_all.astype(jnp.float32)
    grad_stream = cotangent * row_mask
    grad_rows = spread_grads(grad_stream.astype(jnp.bfloat16))
    grad_hidden = jnp.einsum("gd,fd->gf", grad_rows, down_full, preferred_element_type=jnp.float32)
    grad_down = jnp.einsum("gf,gd->fd", hidden, grad_rows, preferred_element_type=jnp.float32)
    unused, gelu_back = jax.vjp(exact_gelu, pre_act)
    grad_pre = gelu_back(grad_hidden)[0].astype(jnp.bfloat16)
    grad_up = jnp.einsum("gd,gf->df", normed_mlp, grad_pre, preferred_element_type=jnp.float32)
    grad_normed = settle_grads(
        jnp.einsum("gf,df->gd", grad_pre, up_full, preferred_element_type=jnp.float32)
    )
    grad_part, gain_mlp = norm_back(after_space, gain_rows[2], grad_normed)
    grad_stream = grad_stream + grad_part
    grad_blended, grad_space_out = out_back(blended_space, space_out, grad_stream)
    grad_mixed = space_view(grad_blended)
    space_weights = jnp.exp(space_scores(query_space, key_space) - space_totals[..., None])
    grad_weights = jnp.einsum(
        "fphd,fqhd->fhpq", grad_mixed, value_space, preferred_element_type=jnp.float32
    )
    row_terms = jnp.sum(space_weights * grad_weights, -1, keepdims=True)
    grad_scores = (space_weights * (grad_weights - row_terms)).astype(jnp.bfloat16)
    grad_query = (
        jnp.einsum("fhpq,fqhd->fphd", grad_scores, key_space, preferred_element_type=jnp.float32)
        * score_scale
    )
    grad_key = (
        jnp.einsum("fhpq,fphd->fqhd", grad_scores, query_space, preferred_element_type=jnp.float32)
        * score_scale
    )
    grad_value = jnp.einsum(
        "fhpq,fphd->fqhd",
        space_weights.astype(jnp.bfloat16),
        grad_mixed,
        preferred_element_type=jnp.float32,
    )
    grad_heads = (
        jnp.stack([grad_query, grad_key, grad_value])
        .astype(jnp.bfloat16)
        .reshape(3, group_count, width_local)
    )
    grad_normed, grad_space_in = heads_back(normed_space, space_in, grad_heads)
    grad_part, gain_space = norm_back(after_time, gain_rows[1], settle_grads(grad_normed))
    grad_stream = grad_stream + grad_part
    grad_blended, grad_time_out = out_back(blended_time, time_out, grad_stream)
    grad_mixed = time_view(grad_blended, slots)
    time_weights = jnp.exp(time_scores(query_time, key_both) - time_totals[..., None])
    grad_weights = jnp.einsum(
        "sfphd,sgphd->sphfg", grad_mixed, value_both, preferred_element_type=jnp.float32
    )
    row_terms = jnp.sum(time_weights * grad_weights, -1)
    grad_scores = (time_weights * (grad_weights - row_terms[..., None])).astype(jnp.bfloat16)
    weights_low = time_weights.astype(jnp.bfloat16)
    grad_query = (
        jnp.einsum("sphfg,sgphd->sfphd", grad_scores, key_both, preferred_element_type=jnp.float32)
        * score_scale
    )
    grad_key_both = time_key_grad(grad_scores, query_time)
    grad_value_both = time_value_grad(weights_low, grad_mixed)
    key_return, value_return = (
        partner(grad_key_both[:, HALF:].astype(jnp.bfloat16), "dp", 0).astype(jnp.float32),
        partner(grad_value_both[:, HALF:].astype(jnp.bfloat16), "dp", 0).astype(jnp.float32),
    )
    grad_key = grad_key_both[:, :HALF] + key_return
    grad_value = grad_value_both[:, :HALF] + value_return
    grad_heads = (
        jnp.stack([grad_query, grad_key, grad_value])
        .astype(jnp.bfloat16)
        .reshape(3, group_count, width_local)
    )
    grad_normed, grad_time_in = heads_back(normed_time, time_in, grad_heads)
    grad_part, gain_time = norm_back(tokens, gain_rows[0], settle_grads(grad_normed))
    grad_tokens = grad_stream + grad_part
    gain_total = lax.psum(jnp.stack([gain_time, gain_space, gain_mlp]), "tensor")
    summed = (
        lax.psum_scatter(gain_total, "dp", scatter_dimension=1, tiled=True),
        lax.psum_scatter(grad_time_in, "dp", scatter_dimension=1, tiled=True),
        lax.psum_scatter(grad_time_out, "dp", scatter_dimension=1, tiled=True),
        lax.psum_scatter(grad_space_in, "dp", scatter_dimension=1, tiled=True),
        lax.psum_scatter(grad_space_out, "dp", scatter_dimension=1, tiled=True),
        lax.psum_scatter(grad_up, "dp", scatter_dimension=0, tiled=True),
        lax.psum_scatter(grad_down, "dp", scatter_dimension=1, tiled=True),
    )
    return (
        output,
        grad_tokens,
        summed[0],
        summed[1],
        summed[2],
        summed[3],
        summed[4],
        summed[5],
        summed[6],
    )


def solution(mesh):
    in_specs = (
        P(("dp", "tensor"), None),
        P("dp"),
        P(None, "dp"),
        P(None, "dp", "tensor"),
        P("tensor", "dp"),
        P(None, "dp", "tensor"),
        P("tensor", "dp"),
        P("dp", "tensor"),
        P("tensor", "dp"),
        P(("dp", "tensor"), None),
    )
    out_specs = (
        P(("dp", "tensor"), None),
        P(("dp", "tensor"), None),
        P(None, "dp"),
        P(None, "dp", "tensor"),
        P("tensor", "dp"),
        P(None, "dp", "tensor"),
        P("tensor", "dp"),
        P("dp", "tensor"),
        P("tensor", "dp"),
    )
    return jax.shard_map(
        on_device, mesh=mesh, in_specs=in_specs, out_specs=out_specs, check_vma=False
    )
```

profile of v0, /device:TPU:0, one launch (start us, length us, event | category | flops | bytes accessed | tf_op | source)
XLA Modules:
  0.0 1167.4 jit_solution(4498531843043997556)
XLA Ops:
  11.8 10.4 all-gather
  23.6 14.3 %all_gather.48 = bf16[3,768,192]{2,0,1:T(4,128)(2,1)} all-gather(bf16[3,96,192]{2,0,1:T(4,128)(2,1)S(1)} %copy.124), channel_id=1, replica_groups=mesh['dp'=8,'tensor'=4] {'dp'}, dimensions={1}, use_global_device_ids=true | all-gather | bytes 995328 | tf_op jit(solution)/shard_map/all_gather | solution.py:135
  40.5 34.2 %all-gather.10.cloned.1.call-done = bf16[1568,768]{1,0:T(8,128)(2,1)} async-done(((bf16[392,768]{1,0:T(8,128)(2,1)}), bf16[1568,768]{1,0:T(8,128)(2,1)}) %all-gather.10.cloned.1.call-update) | async-done | bytes 2408464 | tf_op jit(solution)/shard_map/all_gather | solution.py:41
  80.6 9.8 all_gather.49
  96.5 4.4 reshape_squeeze.19
  109.6 4.4 reshape.181
  117.6 4.4 reshape.182
  122.0 4.0 copy.129
  126.0 4.4 multiply_reduce_fusion.3
  144.8 46.7 %reduce-scatter.24.cloned.1.call-done = bf16[392,768]{1,0:T(8,128)(2,1)} async-done(((bf16[1568,768]{1,0:T(8,128)(2,1)}), bf16[392,768]{1,0:T(8,128)(2,1)}) %reduce-scatter.24.cloned.1.call-update) | async-done | bytes 602128 | tf_op jit(solution)/shard_map/reduce_scatter | solution.py:45
  194.5 13.1 %all_gather.51 = bf16[3,768,192]{2,0,1:T(4,128)(2,1)S(1)} all-gather(bf16[3,96,192]{2,0,1:T(4,128)(2,1)S(1)} %copy.133), channel_id=1, replica_groups=mesh['dp'=8,'tensor'=4] {'dp'}, dimensions={1}, use_global_device_ids=true | all-gather | bytes 995328 | tf_op jit(solution)/shard_map/all_gather | solution.py:137
  209.6 8.5 all_gather.52
  218.0 26.6 %all-gather.12.cloned.1.call-done = bf16[1568,768]{1,0:T(8,128)(2,1)} async-done(((bf16[392,768]{1,0:T(8,128)(2,1)}), bf16[1568,768]{1,0:T(8,128)(2,1)}) %all-gather.12.cloned.1.call-update) | async-done | bytes 2408464 | tf_op jit(solution)/shard_map/all_gather | solution.py:41
  268.7 47.1 %reduce-scatter.26.cloned.1.call-done = bf16[392,768]{1,0:T(8,128)(2,1)} async-done(((bf16[1568,768]{1,0:T(8,128)(2,1)}), bf16[392,768]{1,0:T(8,128)(2,1)}) %reduce-scatter.26.cloned.1.call-update) | async-done | bytes 602128 | tf_op jit(solution)/shard_map/reduce_scatter | solution.py:45
  322.0 46.6 %all-gather.14.cloned.1.call-done = bf16[1568,768]{1,0:T(8,128)(2,1)} async-done(((bf16[392,768]{1,0:T(8,128)(2,1)}), bf16[1568,768]{1,0:T(8,128)(2,1)}) %all-gather.14.cloned.1.call-update) | async-done | bytes 2408464 | tf_op jit(solution)/shard_map/all_gather | solution.py:41
  368.6 6.2 fusion.78
  374.8 18.1 %all-gather.18.cloned.1.call-done = bf16[768,768]{0,1:T(8,128)(2,1)} async-done(((bf16[768,96]{0,1:T(8,128)(2,1)}), bf16[768,768]{0,1:T(8,128)(2,1)}) %all-gather.18.cloned.1.call-update) | async-done | bytes 1179664 | tf_op jit(solution)/shard_map/all_gather | solution.py:140
  392.9 52.3 %all-gather.20.cloned.1.call-done = bf16[1568,768]{1,0:T(8,128)(2,1)} async-done(((bf16[392,768]{1,0:T(8,128)(2,1)}), bf16[1568,768]{1,0:T(8,128)(2,1)}) %all-gather.20.cloned.1.call-update) | async-done | bytes 2408464 | tf_op jit(solution)/shard_map/all_gather | solution.py:51
  445.2 15.5 %add_convert_fusion = (bf16[1568,768]{1,0:T(8,128)(2,1)S(1)}, f32[1568,768]{1,0:T(8,128)}) fusion(f32[1568,768]{1,0:T(8,128)} %fusion.78, bf16[1568,768]{1,0:T(8,128)(2,1)} %all-gather.20.cloned.1.call-done, bf16[768,768]{0,1:T(8,128)(2,1)} %all-gather.18.cloned.1.call-done), kind=kOutput, calls=%fused_computation.8 | convolution fusion | flops 1936392192 | bytes 15630336 | tf_op jit(solution)/shard_map/gd,fd->gf/dot_general | solution.py:206
  465.7 4.6 multiply_convert_fusion.1
  475.4 37.7 %reduce-scatter.30.cloned.1.call-done = bf16[392,768]{1,0:T(8,128)(2,1)} async-done(((bf16[1568,768]{1,0:T(8,128)(2,1)}), bf16[392,768]{1,0:T(8,128)(2,1)}) %reduce-scatter.30.cloned.1.call-update) | async-done | bytes 602128 | tf_op jit(solution)/shard_map/reduce_scatter | solution.py:55
  516.4 47.1 %reduce-scatter.28.cloned.1.call-done = bf16[392,768]{1,0:T(8,128)(2,1)} async-done(((bf16[1568,768]{1,0:T(8,128)(2,1)}), bf16[392,768]{1,0:T(8,128)(2,1)}) %reduce-scatter.28.cloned.1.call-update) | async-done | bytes 602128 | tf_op jit(solution)/shard_map/reduce_scatter | solution.py:45
  567.4 50.4 %all-gather.22.cloned.1.call-done = bf16[1568,768]{1,0:T(8,128)(2,1)} async-done(((bf16[392,768]{1,0:T(8,128)(2,1)}), bf16[1568,768]{1,0:T(8,128)(2,1)}) %all-gather.22.cloned.1.call-update) | async-done | bytes 2408464 | tf_op jit(solution)/shard_map/all_gather | solution.py:51
  627.6 4.0 multiply_reduce_fusion
  647.7 47.5 %reduce-scatter.32.cloned.1.call-done = bf16[392,768]{1,0:T(8,128)(2,1)} async-done(((bf16[1568,768]{1,0:T(8,128)(2,1)}), bf16[392,768]{1,0:T(8,128)(2,1)}) %reduce-scatter.32.cloned.1.call-update) | async-done | bytes 602128 | tf_op jit(solution)/shard_map/reduce_scatter | solution.py:55
  700.6 50.1 %all-gather.24.cloned.1.call-done = bf16[1568,768]{1,0:T(8,128)(2,1)} async-done(((bf16[392,768]{1,0:T(8,128)(2,1)}), bf16[1568,768]{1,0:T(8,128)(2,1)}) %all-gather.24.cloned.1.call-update) | async-done | bytes 2408464 | tf_op jit(solution)/shard_map/all_gather | solution.py:51
  754.1 4.5 reshape.186
  762.4 6.7 multiply_reduce_fusion.2
  769.1 4.6 fusion.49
  773.7 4.1 copy.159
  779.0 6.7 multiply_convert_fusion.3
  790.0 4.1 copy.156
  814.3 5.4 bitcast_convert_fusion
  822.9 5.6 fusion.18
  834.4 3.9 convolution_bitcast_fusion.1
  838.7 4.0 fusion.15
  845.5 4.8 reshape.201
  850.4 16.8 %reduce-scatter.34.cloned.1.call-done = bf16[392,768]{1,0:T(8,128)(2,1)} async-done(((bf16[1568,768]{1,0:T(8,128)(2,1)}), bf16[392,768]{1,0:T(8,128)(2,1)}) %reduce-scatter.34.cloned.1.call-update) | async-done | bytes 602128 | tf_op jit(solution)/shard_map/reduce_scatter | solution.py:55
  871.5 6.2 fusion.81
  877.8 6.3 fusion.80
  884.1 20.4 %reduce-scatter.46.cloned.1.call-done = f32[96,192]{1,0:T(8,128)} async-done(((f32[768,192]{1,0:T(8,128)}), f32[96,192]{1,0:T(8,128)}) %reduce-scatter.46.cloned.1.call-update) | async-done | bytes 73744
  906.2 41.9 %reduce-scatter.44.cloned.1.call-done = f32[96,576]{1,0:T(8,128)} async-done(((f32[768,576]{1,0:T(8,128)}), f32[96,576]{1,0:T(8,128)}) %reduce-scatter.44.cloned.1.call-update) | async-done | bytes 221200
  950.0 36.6 %reduce-scatter.42.cloned.1.call-done = f32[96,192]{1,0:T(8,128)} async-done(((f32[768,192]{1,0:T(8,128)}), f32[96,192]{1,0:T(8,128)}) %reduce-scatter.42.cloned.1.call-update) | async-done | bytes 73744
  988.3 41.9 %reduce-scatter.40.cloned.1.call-done = f32[96,576]{1,0:T(8,128)} async-done(((f32[768,576]{1,0:T(8,128)}), f32[96,576]{1,0:T(8,128)}) %reduce-scatter.40.cloned.1.call-update) | async-done | bytes 221200
  1034.9 32.1 %reduce-scatter.48.cloned.1.call-done = f32[96,3]{1,0:T(8,128)} async-done(((f32[768,3]{1,0:T(8,128)}), f32[96,3]{1,0:T(8,128)}) %reduce-scatter.48.cloned.1.call-update) | async-done | bytes 1168
  1067.9 12.2 %psum.8 = f32[3,96]{1,0:T(4,128)} all-reduce(f32[3,96]{1,0:T(4,128)S(1)} %copy.177), channel_id=1, replica_groups=mesh['dp'=8,'tensor'=4] {'tensor'}, use_global_device_ids=true, to_apply=%region_27.28 | all-reduce | flops 288 | bytes 2304 | tf_op jit(solution)/shard_map/psum | solution.py:275
  1080.1 33.1 %reduce-scatter.38.cloned.1.call-done = f32[768,96]{0,1:T(8,128)} async-done(((f32[768,768]{0,1:T(8,128)}), f32[768,96]{0,1:T(8,128)}) %reduce-scatter.38.cloned.1.call-update) | async-done | bytes 294928 | tf_op jit(solution)/shard_map/reduce_scatter | solution.py:283
  1113.2 46.2 %reduce-scatter.36.cloned.1.call-done = f32[96,768]{1,0:T(8,128)} async-done(((f32[768,768]{1,0:T(8,128)}), f32[96,768]{1,0:T(8,128)}) %reduce-scatter.36.cloned.1.call-update) | async-done | bytes 294928 | tf_op jit(solution)/shard_map/reduce_scatter | solution.py:282
  (287 shorter events, 189.0 us)
Async XLA Ops:
  8.0 14.3 %copy-start.1 = (f32[392,768]{1,0:T(8,128)S(1)}, f32[392,768]{1,0:T(8,128)}, u32[]{:S(2)}) copy-start(f32[392,768]{1,0:T(8,128)} %param.10) | copy-start | bytes 3612676
  8.0 15.4 %copy-start.38 = (bf16[3,96,192]{2,1,0:T(8,128)(2,1)S(1)}, bf16[3,96,192]{2,1,0:T(8,128)(2,1)}, u32[]{:S(2)}) copy-start(bf16[3,96,192]{2,1,0:T(8,128)(2,1)} %param.13) | copy-start | bytes 331780
  8.0 66.7 %all-gather.10.cloned.1.call-start = ((), (), s32[]{:S(2)}) async-start(), calls=%async_computation.13 | async-start | bytes 3010560 | tf_op jit(solution)/shard_map/all_gather | solution.py:41
  9.6 28.3 %copy-start.42 = (f32[392]{0:T(512)}, f32[392]{0:T(512)S(1)}, u32[]{:S(2)}) copy-start(f32[392]{0:T(512)S(1)} %broadcast_multiply_fusion.2) | copy-start | bytes 4708
  11.8 28.7 %copy-start.46 = (f32[392]{0:T(512)}, f32[392]{0:T(512)S(1)}, u32[]{:S(2)}) copy-start(f32[392]{0:T(512)S(1)} %fusion.58) | copy-start | bytes 4708
  23.4 168.1 %reduce-scatter.24.cloned.1.call-start = ((), (), s32[]{:S(2)}) async-start(), calls=%async_computation.14 | async-start | bytes 3010560 | tf_op jit(solution)/shard_map/reduce_scatter | solution.py:45
  40.5 37.7 %copy-start.35 = (bf16[3,768,192]{1,2,0:T(8,128)(2,1)}, bf16[3,768,192]{1,2,0:T(8,128)(2,1)S(1)}, u32[]{:S(2)}) copy-start(bf16[3,768,192]{1,2,0:T(8,128)(2,1)S(1)} %copy.125) | copy-start | bytes 2654212
  80.0 29.6 %collective-permute-start = (bf16[1568,192]{0,1:T(8,128)(2,1)}, bf16[1568,192]{0,1:T(8,128)(2,1)}, u32[]{:S(2)}, u32[]{:S(2)}) collective-permute-start(bf16[1568,192]{0,1:T(8,128)(2,1)} %get-tuple-element.68), channel_id=1, source_target_pairs={{0,4},{4,0},{8,12},{12,8},{16,20},{20,16},{24,28},{28,24},{1,5},{5... | collective-permute-start | bytes 1806344 | tf_op jit(solution)/shard_map/ppermute | solution.py:21
  80.0 37.6 %collective-permute-start.1 = (bf16[1568,192]{0,1:T(8,128)(2,1)}, bf16[1568,192]{0,1:T(8,128)(2,1)}, u32[]{:S(2)}, u32[]{:S(2)}) collective-permute-start(bf16[1568,192]{0,1:T(8,128)(2,1)} %get-tuple-element.69), channel_id=1, source_target_pairs={{0,4},{4,0},{8,12},{12,8},{16,20},{20,16},{24,28},{28,24},{1,5},{5... | collective-permute-start | bytes 1806344 | tf_op jit(solution)/shard_map/ppermute | solution.py:21
  90.4 52.0 %copy-start.19 = (bf16[192,768]{0,1:T(8,128)(2,1)}, bf16[192,768]{0,1:T(8,128)(2,1)S(1)}, u32[]{:S(2)}) copy-start(bf16[192,768]{0,1:T(8,128)(2,1)S(1)} %all_gather.49) | copy-start | bytes 884740
  103.8 22.2 %copy-start.15 = (bf16[2,4,196,3,64]{4,1,3,2,0:T(4,128)(2,1)}, bf16[2,4,196,3,64]{4,1,3,2,0:T(4,128)(2,1)S(1)}, u32[]{:S(2)}) copy-start(bf16[2,4,196,3,64]{4,1,3,2,0:T(4,128)(2,1)S(1)} %copy.130) | copy-start | bytes 1806340
  144.7 99.9 %all-gather.12.cloned.1.call-start = ((), (), s32[]{:S(2)}) async-start(), calls=%async_computation.15 | async-start | bytes 3010560 | tf_op jit(solution)/shard_map/all_gather | solution.py:41
  194.2 121.6 %reduce-scatter.26.cloned.1.call-start = ((), (), s32[]{:S(2)}) async-start(), calls=%async_computation.16 | async-start | bytes 3010560 | tf_op jit(solution)/shard_map/reduce_scatter | solution.py:45
  218.0 47.6 %copy-start.21 = (bf16[192,768]{0,1:T(8,128)(2,1)}, bf16[192,768]{0,1:T(8,128)(2,1)S(1)}, u32[]{:S(2)}) copy-start(bf16[192,768]{0,1:T(8,128)(2,1)S(1)} %all_gather.52) | copy-start | bytes 884740
  268.0 54.0 %all-gather.16.cloned.1.call-start = ((), (), s32[]{:S(2)}) async-start(), calls=%async_computation.18 | async-start | bytes 1327104 | tf_op jit(solution)/shard_map/all_gather | solution.py:139
  268.6 100.0 %all-gather.14.cloned.1.call-start = ((), (), s32[]{:S(2)}) async-start(), calls=%async_computation.17 | async-start | bytes 3010560 | tf_op jit(solution)/shard_map/all_gather | solution.py:41
  318.4 74.5 %all-gather.18.cloned.1.call-start = ((), (), s32[]{:S(2)}) async-start(), calls=%async_computation.19 | async-start | bytes 1327104 | tf_op jit(solution)/shard_map/all_gather | solution.py:140
  319.0 126.2 %all-gather.20.cloned.1.call-start = ((), (), s32[]{:S(2)}) async-start(), calls=%async_computation.21 | async-start | bytes 3010560 | tf_op jit(solution)/shard_map/all_gather | solution.py:51
  321.9 191.2 %reduce-scatter.30.cloned.1.call-start = ((), (), s32[]{:S(2)}) async-start(), calls=%async_computation.22 | async-start | bytes 3010560 | tf_op jit(solution)/shard_map/reduce_scatter | solution.py:55
  445.2 16.9 %copy-start.51 = (bf16[768,768]{1,0:T(8,128)(2,1)S(1)}, bf16[768,768]{1,0:T(8,128)(2,1)}, u32[]{:S(2)}) copy-start(bf16[768,768]{1,0:T(8,128)(2,1)} %all-gather.16.cloned.1.call-done) | copy-start | bytes 3538948
  465.6 97.8 %reduce-scatter.28.cloned.1.call-start = ((), (), s32[]{:S(2)}) async-start(), calls=%async_computation.20 | async-start | bytes 3010560 | tf_op jit(solution)/shard_map/reduce_scatter | solution.py:45
  475.3 142.4 %all-gather.22.cloned.1.call-start = ((), (), s32[]{:S(2)}) async-start(), calls=%async_computation.23 | async-start | bytes 3010560 | tf_op jit(solution)/shard_map/all_gather | solution.py:51
  567.4 127.9 %reduce-scatter.32.cloned.1.call-start = ((), (), s32[]{:S(2)}) async-start(), calls=%async_computation.24 | async-start | bytes 3010560 | tf_op jit(solution)/shard_map/reduce_scatter | solution.py:55
  624.1 7.6 slice-start
  647.5 52.0 %copy-start.3 = (f32[392,768]{1,0:T(8,128)S(1)}, f32[392,768]{1,0:T(8,128)}, u32[]{:S(2)}) copy-start(f32[392,768]{1,0:T(8,128)} %get-tuple-element.57) | copy-start | bytes 3612676
  647.5 103.2 %all-gather.24.cloned.1.call-start = ((), (), s32[]{:S(2)}) async-start(), calls=%async_computation.25 | async-start | bytes 3010560 | tf_op jit(solution)/shard_map/all_gather | solution.py:51
  698.4 52.3 %copy-start.20 = (bf16[192,768]{0,1:T(8,128)(2,1)S(1)}, bf16[192,768]{0,1:T(8,128)(2,1)}, u32[]{:S(2)}) copy-start(bf16[192,768]{0,1:T(8,128)(2,1)} %copy-done.19) | copy-start | bytes 884740
  700.5 166.7 %reduce-scatter.34.cloned.1.call-start = ((), (), s32[]{:S(2)}) async-start(), calls=%async_computation.26 | async-start | bytes 3010560 | tf_op jit(solution)/shard_map/reduce_scatter | solution.py:55
  754.1 8.2 copy-start.10
  754.1 8.2 copy-start.23
  777.8 7.8 copy-start.8
  779.0 24.1 %collective-permute-start.3 = (bf16[2,4,196,3,64]{2,4,3,1,0:T(8,128)(2,1)}, bf16[2,4,196,3,64]{2,4,3,1,0:T(8,128)(2,1)}, u32[]{:S(2)}, u32[]{:S(2)}) collective-permute-start(bf16[2,4,196,3,64]{2,4,3,1,0:T(8,128)(2,1)} %slice.85), channel_id=1, source_target_pairs={{0,4},{4,0},{8,12},{12,8},{16,20},{20,16},{24,28},{28,24},{1,5},{5... | collective-permute-start | bytes 1806344 | tf_op jit(solution)/shard_map/ppermute | solution.py:21
  779.0 7.7 copy-start.16
  797.1 12.5 %collective-permute-start.2 = (bf16[2,4,196,3,64]{2,4,3,1,0:T(8,128)(2,1)}, bf16[2,4,196,3,64]{2,4,3,1,0:T(8,128)(2,1)}, u32[]{:S(2)}, u32[]{:S(2)}) collective-permute-start(bf16[2,4,196,3,64]{2,4,3,1,0:T(8,128)(2,1)} %slice.86), channel_id=1, source_target_pairs={{0,4},{4,0},{8,12},{12,8},{16,20},{20,16},{24,28},{28,24},{1,5},{5... | collective-permute-start | bytes 1806344 | tf_op jit(solution)/shard_map/ppermute | solution.py:21
  819.7 84.9 %reduce-scatter.46.cloned.1.call-start = ((), (), s32[]{:S(2)}) async-start(), calls=%async_computation.32 | async-start | bytes 884736
  822.8 125.3 %reduce-scatter.44.cloned.1.call-start = ((), (), s32[]{:S(2)}) async-start(), calls=%async_computation.31 | async-start | bytes 2211840
  834.4 152.3 %reduce-scatter.42.cloned.1.call-start = ((), (), s32[]{:S(2)}) async-start(), calls=%async_computation.30 | async-start | bytes 884736
  838.4 191.8 %reduce-scatter.40.cloned.1.call-start = ((), (), s32[]{:S(2)}) async-start(), calls=%async_computation.29 | async-start | bytes 2211840
  845.5 21.7 %copy-start.2 = (f32[392,768]{1,0:T(8,128)S(1)}, f32[392,768]{1,0:T(8,128)}, u32[]{:S(2)}) copy-start(f32[392,768]{1,0:T(8,128)} %param.10) | copy-start | bytes 3612676
  845.5 21.7 %copy-start.41 = (f32[768]{0:T(1024)S(1)}, f32[768]{0:T(1024)}, u32[]{:S(2)}) copy-start(f32[768]{0:T(1024)} %copy-done.40) | copy-start | bytes 9220
  845.5 21.7 %copy-start.43 = (f32[392]{0:T(512)S(1)}, f32[392]{0:T(512)}, u32[]{:S(2)}) copy-start(f32[392]{0:T(512)} %copy-done.42) | copy-start | bytes 4708
  850.3 18.3 %copy-start.49 = (f32[392]{0:T(512)S(1)}, f32[392]{0:T(512)}, u32[]{:S(2)}) copy-start(f32[392]{0:T(512)} %copy-done.48) | copy-start | bytes 4708
  850.3 18.3 %copy-start.47 = (f32[392]{0:T(512)S(1)}, f32[392]{0:T(512)}, u32[]{:S(2)}) copy-start(f32[392]{0:T(512)} %copy-done.46) | copy-start | bytes 4708
  850.4 216.7 %reduce-scatter.48.cloned.1.call-start = ((), (), s32[]{:S(2)}) async-start(), calls=%async_computation.33 | async-start | bytes 442368
  871.4 241.8 %reduce-scatter.38.cloned.1.call-start = ((), (), s32[]{:S(2)}) async-start(), calls=%async_computation.28 | async-start | bytes 2654208 | tf_op jit(solution)/shard_map/reduce_scatter | solution.py:283
  877.7 281.7 %reduce-scatter.36.cloned.1.call-start = ((), (), s32[]{:S(2)}) async-start(), calls=%async_computation.27 | async-start | bytes 2654208 | tf_op jit(solution)/shard_map/reduce_scatter | solution.py:282
  884.1 148.0 %copy-start.4 = (f32[392,768]{1,0:T(8,128)S(1)}, f32[392,768]{1,0:T(8,128)}, u32[]{:S(2)}) copy-start(f32[392,768]{1,0:T(8,128)} %get-tuple-element.57) | copy-start | bytes 3612676
  884.1 148.0 %copy-start.14 = (bf16[392,768]{1,0:T(8,128)(2,1)S(1)}, bf16[392,768]{1,0:T(8,128)(2,1)}, u32[]{:S(2)}) copy-start(bf16[392,768]{1,0:T(8,128)(2,1)} %reduce-scatter.34.cloned.1.call-done) | copy-start | bytes 1806340
  (33 other events, 93.4 us)
Sparse Core Ops, SparseCore 0:
  23.5 51.1 all-gather.9
  144.8 46.6 reduce-scatter.23
  194.3 50.3 all-gather.11
  268.1 47.5 reduce-scatter.25
  567.5 50.2 all-gather.21
  647.6 47.5 reduce-scatter.31
Sparse Core Ops, SparseCore 1:
  270.4 22.4 all-gather.15
  318.5 50.0 all-gather.13
  370.3 22.5 all-gather.17
  394.5 50.6 all-gather.19
  465.7 47.4 reduce-scatter.29
  515.5 48.0 reduce-scatter.27
  700.6 50.0 all-gather.23
  819.8 47.4 reduce-scatter.33
  870.2 34.3 reduce-scatter.45
  908.0 40.0 reduce-scatter.43
  951.7 34.9 reduce-scatter.41
  990.1 40.0 reduce-scatter.39
  1033.1 33.9 reduce-scatter.47
  1071.0 42.2 reduce-scatter.37
  1117.2 42.2 reduce-scatter.35
where the time goes:
time: 1170 us
  waiting for transfers between devices  775 us (66%)
  local copies, waits for them, and re-layouts  131 us (11%)
  matrix products  123 us (11%)
  blocking collectives  68.2 us (6%)
  other arithmetic  50 us (4%)
  between operations  18 us (2%)
    unnamed x26, waiting for transfers between devices  174 us
    all_gather x3, waiting for transfers between devices, spread_grads(): return lax.all_gather(local_part, 'tensor', axis=0, tiled=True)  153 us
    reduce_scatter x3, waiting for transfers between devices, settle_rows(): lax.psum_scatter(partial_sum.astype(jnp.bfloat16), 'tensor', scatter_dime...  141 us
    all_gather x3, waiting for transfers between devices, spread_rows(): return lax.all_gather(local_part, 'tensor', axis=0, tiled=True)  107 us
    reduce_scatter x3, waiting for transfers between devices, settle_grads(): lax.psum_scatter(partial_sum.astype(jnp.bfloat16), 'tensor', scatter_dime...  102 us
    reduce_scatter x1, waiting for transfers between devices, on_device(): lax.psum_scatter(grad_up, 'dp', scatter_dimension=0, tiled=True)  46.2 us
    unnamed x132, local copies, waits for them, and re-layouts  37.7 us
    reduce_scatter x1, waiting for transfers between devices, on_device(): lax.psum_scatter(grad_down, 'dp', scatter_dimension=1, tiled=True)  33.1 us
  transfers between devices with their start and end apart: 25, of which 20 were waited for; matrix products, arithmetic and copies ran while one was open for 12% of the time, Pallas kernels for 0%

commit v1 on v0

v1 whole, which is shorter than its diff:
```python
import functools

import jax
import jax.numpy as jnp
from jax import lax
from jax.experimental import pallas as pl
from jax.experimental.pallas import tpu as pltpu
from jax.sharding import Mesh, PartitionSpec as P

HEAD_DIM = 64
PATCHES = 196
HALF = 4
FRAMES = 8
EPSILON = 1e-06
F32 = jnp.float32
BF16 = jnp.bfloat16
ALL = ("o", "c", "s", "h")
DP = ("o", "c")
TENSOR = ("s", "h")
CLIP = ("c", "h")

NN = (((1,), (0,)), ((), ()))
NT = (((1,), (1,)), ((), ()))


def mm(a, b, dims=NN):
    return lax.dot_general(a, b, dims, preferred_element_type=F32)


def row_ids(shape, dim, start):
    return lax.broadcasted_iota(jnp.int32, shape, dim) + start


def windows(kind, count):
    if kind == "time":
        return [(0, count, None)]
    found = []
    for frame in range(count // PATCHES):
        low = frame * PATCHES // 16 * 16
        high = min(count, -(-(frame + 1) * PATCHES // 16) * 16)
        found.append((low, high - low, frame))
    return found


def key_bias(start, size, group, stride):
    keys = row_ids((size, size), 0, start)
    if group is None:
        together = keys % stride == row_ids((size, size), 1, start) % stride
    else:
        together = (keys >= group * PATCHES) & (keys < (group + 1) * PATCHES)
    return jnp.where(together, 0.0, -1e30)


def row_valid(start, size, group, width):
    rows = row_ids((size, width), 0, start)
    return (rows >= group * PATCHES) & (rows < (group + 1) * PATCHES)


def attend_kernel(kind, stride, heads_ref, mixed_ref, sums):
    count = heads_ref.shape[0]
    width = mixed_ref.shape[1]
    sums[...] = jnp.zeros_like(sums)
    for start, size, group in windows(kind, count):
        bias = key_bias(start, size, group, stride)
        rows = pl.ds(start, size)
        for head in range(width // HEAD_DIM):
            low = head * HEAD_DIM
            query = heads_ref[rows, low : low + HEAD_DIM] * HEAD_DIM**-0.5
            key = heads_ref[rows, width + low : width + low + HEAD_DIM]
            value = heads_ref[rows, 2 * width + low : 2 * width + low + HEAD_DIM]
            scores = mm(key, query, NT) + bias
            weights = jnp.exp(scores - jnp.max(scores, 0, keepdims=True))
            total = jnp.sum(weights, 0, keepdims=True)
            blended = mm(value.T, weights.astype(BF16)) / total
            blended = blended.T
            if group is not None:
                blended = jnp.where(row_valid(start, size, group, HEAD_DIM), blended, 0.0)
            sums[rows, low : low + HEAD_DIM] += blended
    mixed_ref[...] = sums[...].astype(BF16)


def attend_back_kernel(kind, stride, heads_ref, grad_ref, out_ref, sums):
    count = heads_ref.shape[0]
    width = grad_ref.shape[1]
    scale = HEAD_DIM**-0.5
    sums[...] = jnp.zeros_like(sums)
    for start, size, group in windows(kind, count):
        bias = key_bias(start, size, group, stride)
        rows = pl.ds(start, size)
        for head in range(width // HEAD_DIM):
            low = head * HEAD_DIM
            query = heads_ref[rows, low : low + HEAD_DIM] * scale
            key = heads_ref[rows, width + low : width + low + HEAD_DIM]
            value = heads_ref[rows, 2 * width + low : 2 * width + low + HEAD_DIM]
            grad = grad_ref[rows, low : low + HEAD_DIM]
            if group is not None:
                grad = jnp.where(
                    row_valid(start, size, group, HEAD_DIM), grad.astype(F32), 0.0
                ).astype(BF16)
            scores = mm(key, query, NT) + bias
            weights = jnp.exp(scores - jnp.max(scores, 0, keepdims=True))
            weights = weights / jnp.sum(weights, 0, keepdims=True)
            grad_weights = mm(value, grad, NT)
            row_terms = jnp.sum(weights * grad_weights, 0, keepdims=True)
            grad_scores = (weights * (grad_weights - row_terms)).astype(BF16)
            grad_query = (mm(key.T, grad_scores) * scale).T
            grad_key = mm(grad_scores, query)
            grad_value = mm(weights.astype(BF16), grad)
            sums[rows, low : low + HEAD_DIM] += grad_query
            sums[rows, width + low : width + low + HEAD_DIM] += grad_key
            sums[rows, 2 * width + low : 2 * width + low + HEAD_DIM] += grad_value
    out_ref[...] = sums[...].astype(BF16)


def attend(kind, heads, stride=1):
    blocks, count, columns = heads.shape
    width = columns // 3
    spec = lambda lanes: pl.BlockSpec((None, count, lanes), lambda i: (i, 0, 0))
    return pl.pallas_call(
        functools.partial(attend_kernel, kind, stride),
        grid=(blocks,),
        in_specs=[spec(columns)],
        out_specs=spec(width),
        out_shape=jax.ShapeDtypeStruct((blocks, count, width), BF16),
        scratch_shapes=[pltpu.VMEM((count, width), F32)],
        name=kind + "_attend",
    )(heads)


def attend_back(kind, heads, grad, stride=1):
    blocks, count, columns = heads.shape
    width = columns // 3
    spec = lambda lanes: pl.BlockSpec((None, count, lanes), lambda i: (i, 0, 0))
    return pl.pallas_call(
        functools.partial(attend_back_kernel, kind, stride),
        grid=(blocks,),
        in_specs=[spec(columns), spec(width)],
        out_specs=spec(columns),
        out_shape=jax.ShapeDtypeStruct((blocks, count, columns), BF16),
        scratch_shapes=[pltpu.VMEM((count, columns), F32)],
        name=kind + "_attend_back",
    )(heads, grad)


def normalize(rows, scale_row):
    average = jnp.mean(rows, -1, keepdims=True)
    centred = rows - average
    spread = jnp.mean(centred * centred, -1, keepdims=True)
    return centred * lax.rsqrt(spread + EPSILON) * scale_row


def norm_back(rows, scale_row, grad_normed):
    unused, pullback = jax.vjp(normalize, rows, scale_row)
    return pullback(grad_normed)


def gather_weights(shard):
    every = lax.all_gather(shard, TENSOR, axis=0, tiled=False)
    every = every.reshape(-1, *shard.shape)
    return lax.all_gather(every, DP, axis=1, tiled=True)


def reduce_grads(blocks):
    part = lax.psum_scatter(blocks.astype(BF16), TENSOR, scatter_dimension=0, tiled=True)[0]
    return lax.psum_scatter(part, DP, scatter_dimension=0, tiled=True)


def to_patches(rows, members):
    share = PATCHES // members
    columns = rows.shape[1]
    parts = rows.reshape(-1, members, share, columns).transpose(1, 0, 2, 3)
    return lax.all_to_all(parts, CLIP, 0, 0, tiled=True).reshape(-1, columns)


def to_frames(rows, members):
    share = PATCHES // members
    columns = rows.shape[1]
    parts = rows.reshape(members, -1, share, columns)
    parts = lax.all_to_all(parts, CLIP, 0, 0, tiled=True)
    return parts.transpose(1, 0, 2, 3).reshape(-1, columns)


def on_device(
    tokens,
    live_clips,
    norm_gains,
    qkv_time,
    out_time,
    qkv_space,
    out_space,
    up_weight,
    down_weight,
    cotangent,
):
    members = lax.axis_size("c") * lax.axis_size("h")
    share = PATCHES // members
    live = jnp.where(lax.axis_index("s") < live_clips[0], 1.0, 0.0).astype(F32)

    def pack_heads(qkv, out):
        rows = qkv.shape[1]
        return jnp.concatenate([qkv.transpose(1, 0, 2).reshape(rows, -1), out.T], 1)

    time_all = gather_weights(pack_heads(qkv_time, out_time))
    space_all = gather_weights(pack_heads(qkv_space, out_space))
    up_all = gather_weights(up_weight)
    down_all = gather_weights(down_weight.T)
    gains = lax.all_gather(norm_gains, DP, axis=1, tiled=True).astype(F32)
    width = qkv_time.shape[2]
    time_in, time_out = time_all[:, :, : 3 * width], time_all[:, :, 3 * width :]
    space_in, space_out = space_all[:, :, : 3 * width], space_all[:, :, 3 * width :]

    def heads_of(normed, weight):
        return jnp.einsum("gd,tde->tge", normed, weight, preferred_element_type=F32).astype(BF16)

    def project(mixed, weight):
        return jnp.einsum("tge,tne->gn", mixed, weight, preferred_element_type=F32)

    def project_back(grad, weight):
        return jnp.einsum("gn,tne->tge", grad, weight, preferred_element_type=F32)

    def heads_back(grad_heads, weight):
        return jnp.einsum("tge,tde->gd", grad_heads, weight, preferred_element_type=F32)

    def outer(rows, blocks):
        return jnp.einsum("gd,tge->tde", rows, blocks, preferred_element_type=F32)

    normed_time = to_patches(normalize(tokens, gains[0]).astype(BF16), members)
    time_heads = heads_of(normed_time, time_in)
    time_mixed = attend("time", time_heads, share)
    after_time = tokens + to_frames(project(time_mixed, time_out).astype(BF16), members).astype(F32)
    normed_space = normalize(after_time, gains[1]).astype(BF16)
    space_heads = heads_of(normed_space, space_in)
    space_mixed = attend("space", space_heads)
    after_space = after_time + project(space_mixed, space_out)
    normed_mlp = normalize(after_space, gains[2]).astype(BF16)
    pre_act = jnp.einsum("gd,tde->tge", normed_mlp, up_all, preferred_element_type=F32)
    cdf = 0.5 * (1.0 + lax.erf(pre_act * 0.5**0.5))
    hidden = (pre_act * cdf).astype(BF16)
    slope = cdf + pre_act * (jnp.exp(-0.5 * pre_act * pre_act) * (0.5 / jnp.pi) ** 0.5)
    output = (after_space + project(hidden, down_all)) * live

    grad_stream = cotangent * live
    grad_low = grad_stream.astype(BF16)
    grad_down = outer(grad_low, hidden)
    grad_pre = (project_back(grad_low, down_all) * slope).astype(BF16)
    grad_up = outer(normed_mlp, grad_pre)
    grad_part, gain_mlp = norm_back(after_space, gains[2], heads_back(grad_pre, up_all))
    grad_stream = grad_stream + grad_part
    grad_low = grad_stream.astype(BF16)
    grad_space_out = outer(grad_low, space_mixed)
    grad_mixed = project_back(grad_low, space_out).astype(BF16)
    grad_heads = attend_back("space", space_heads, grad_mixed)
    grad_space_in = outer(normed_space, grad_heads)
    grad_part, gain_space = norm_back(after_time, gains[1], heads_back(grad_heads, space_in))
    grad_stream = grad_stream + grad_part
    grad_low = to_patches(grad_stream.astype(BF16), members)
    grad_time_out = outer(grad_low, time_mixed)
    grad_mixed = project_back(grad_low, time_out).astype(BF16)
    grad_heads = attend_back("time", time_heads, grad_mixed, share)
    grad_time_in = outer(normed_time, grad_heads)
    grad_normed = to_frames(heads_back(grad_heads, time_in).astype(BF16), members).astype(F32)
    grad_part, gain_time = norm_back(tokens, gains[0], grad_normed)
    grad_tokens = grad_stream + grad_part

    down_own = reduce_grads(grad_down).T
    up_own = reduce_grads(grad_up)
    space_own = reduce_grads(jnp.concatenate([grad_space_in, grad_space_out], 2))
    time_own = reduce_grads(jnp.concatenate([grad_time_in, grad_time_out], 2))
    gains_own = lax.psum(jnp.stack([gain_time, gain_space, gain_mlp]), TENSOR)
    gains_own = lax.psum_scatter(gains_own, DP, scatter_dimension=1, tiled=True)

    def unpack(own):
        rows = own.shape[0]
        return own[:, : 3 * width].reshape(rows, 3, width).transpose(1, 0, 2), own[:, 3 * width :].T

    time_in_own, time_out_own = unpack(time_own.astype(F32))
    space_in_own, space_out_own = unpack(space_own.astype(F32))
    return (
        output,
        grad_tokens,
        gains_own,
        time_in_own,
        time_out_own,
        space_in_own,
        space_out_own,
        up_own.astype(F32),
        down_own.astype(F32),
    )


def solution(mesh):
    n_dp, n_tensor = mesh.devices.shape

    def run(*args):
        slots = args[0].shape[0] // (n_dp * HALF * PATCHES)
        fine = Mesh(mesh.devices.reshape(n_dp // 2, 2, slots, n_tensor // slots), ALL)
        in_specs = (
            P(ALL, None),
            P(DP),
            P(None, DP),
            P(None, DP, TENSOR),
            P(TENSOR, DP),
            P(None, DP, TENSOR),
            P(TENSOR, DP),
            P(DP, TENSOR),
            P(TENSOR, DP),
            P(ALL, None),
        )
        out_specs = (in_specs[0], in_specs[0]) + in_specs[2:9]
        return jax.shard_map(
            on_device, mesh=fine, in_specs=in_specs, out_specs=out_specs, check_vma=False
        )(*args)

    return run
```

time: 1170 us -> 814 us (0.70)
  waiting for transfers between devices: 775 us -> 427 us
  blocking collectives: 68.2 us -> 130 us
  local copies, waits for them, and re-layouts: 131 us -> 82.6 us
  Pallas kernels: 0 us -> 42.2 us
  matrix products: 123 us -> 83.7 us
  other arithmetic: 50 us -> 15.5 us
    all_gather x8 -> x4, waiting for transfers between devices: 278 us -> 4 us  [gather_weights(): return lax.all_gather(every, DP, axis=1, tiled=True)]
    reduce_scatter x8 -> x4, waiting for transfers between devices: 322 us -> 248 us  [reduce_grads(): lax.psum_scatter(blocks.astype(BF16), TENSOR, scatter_dimension=0, tiled=...]
    pallas_call x0 -> x4, Pallas kernels: none -> 42.2 us  [the longest x2 25.7 us: attend_back(): pl.pallas_call(functools.partial(attend_back_kernel, kind, stride), grid=...]
    all_to_all x0 -> x2, blocking collectives: none -> 40.2 us  [to_patches(): return lax.all_to_all(parts, CLIP, 0, 0, tiled=True).reshape(-1, columns)]
    another operation x19 -> x0, local copies, waits for them, and re-layouts: 37.7 us -> none  [the longest x6 19.2 us: time_view(): return flat.reshape(slots, HALF, PATCHES, -1, HEAD_DIM)]
    dot_general x26 -> x18, matrix products: 110 us -> 83.7 us  [the longest x6 24.6 us: outer(): return jnp.einsum('gd,tge->tde', rows, blocks, preferred_element_type=F32)]
    reshape x12 -> x13, local copies, waits for them, and re-layouts: 30.2 us -> 8.5 us  [the longest x4 4.03 us: to_frames(): parts = rows.reshape(members, -1, share, columns)]
    all_gather x5, blocking collectives: 56 us -> 77.1 us  [the longest x4 68 us: gather_weights(): every = lax.all_gather(shard, TENSOR, axis=0, tiled=False)]
  transfers between devices with their start and end apart: 25 -> 15, of which waited for: 20 -> 10; matrix products, arithmetic and copies ran while one was open for 12% -> 17% of each run, Pallas kernels for 0% -> 4%
where the time goes in v1:
time: 814 us; the launch traced here: 804 us
  waiting for transfers between devices  427 us (52%)
  blocking collectives  130 us (16%)
  matrix products  83.7 us (10%)
  local copies, waits for them, and re-layouts  82.6 us (10%)
  Pallas kernels  42.2 us (5%)
  between operations  15.6 us (2%)
  other arithmetic  15.5 us (2%)
    reduce_scatter x4, waiting for transfers between devices, reduce_grads(): lax.psum_scatter(blocks.astype(BF16), TENSOR, scatter_dimension=0, tiled=...  248 us
    unnamed x18, waiting for transfers between devices  166 us
    all_gather x4, blocking collectives, gather_weights(): every = lax.all_gather(shard, TENSOR, axis=0, tiled=False)  68 us
    unnamed x68, local copies, waits for them, and re-layouts  43.3 us
    all_to_all x2, blocking collectives, to_patches(): return lax.all_to_all(parts, CLIP, 0, 0, tiled=True).reshape(-1, columns)  40.2 us
    pallas_call x2, Pallas kernels, attend_back(): pl.pallas_call(functools.partial(attend_back_kernel, kind, stride), grid=...  25.7 us
    dot_general x6, matrix products, outer(): return jnp.einsum('gd,tge->tde', rows, blocks, preferred_element_type=F32)  24.6 us
    dot_general x3, matrix products, project_back(): return jnp.einsum('gn,tne->tge', grad, weight, preferred_element_type=F32)  21.3 us
  transfers between devices with their start and end apart: 15, of which 10 were waited for; matrix products, arithmetic and copies ran while one was open for 17% of the time, Pallas kernels for 4%

profile of v1, /device:TPU:0, one launch (start us, length us, event | category | flops | bytes accessed | tf_op | source)
XLA Modules:
  0.0 804.5 jit_solution(9590935782418432623)
XLA Ops:
  9.3 18.4 %all-gather = bf16[384,768]{1,0:T(8,128)(2,1)S(1)} all-gather(bf16[96,768]{1,0:T(8,128)(2,1)S(1)} %copy.86), channel_id=2, replica_groups=mesh['o'=4,'c'=2,'s'=2,'h'=2] {'s','h'}, dimensions={0}, use_global_device_ids=true | all-gather | bytes 737280 | tf_op jit(solution)/shard_map/all_gather | solution.py:158
  29.4 16.3 %all-gather.1 = bf16[384,768]{1,0:T(8,128)(2,1)S(1)} all-gather(bf16[96,768]{1,0:T(8,128)(2,1)S(1)} %copy.97), channel_id=3, replica_groups=mesh['o'=4,'c'=2,'s'=2,'h'=2] {'s','h'}, dimensions={0}, use_global_device_ids=true | all-gather | bytes 737280 | tf_op jit(solution)/shard_map/all_gather | solution.py:158
  47.1 17.5 %all-gather.2 = bf16[384,768]{1,0:T(8,128)(2,1)} all-gather(bf16[96,768]{1,0:T(8,128)(2,1)S(1)} %copy-done.20), channel_id=4, replica_groups=mesh['o'=4,'c'=2,'s'=2,'h'=2] {'s','h'}, dimensions={0}, use_global_device_ids=true | all-gather | bytes 737280 | tf_op jit(solution)/shard_map/all_gather | solution.py:158
  64.7 15.8 %all-gather.3 = bf16[384,768]{1,0:T(8,128)(2,1)} all-gather(bf16[96,768]{1,0:T(8,128)(2,1)S(1)} %bitcast.171), channel_id=5, replica_groups=mesh['o'=4,'c'=2,'s'=2,'h'=2] {'s','h'}, dimensions={0}, use_global_device_ids=true | all-gather | bytes 737280 | tf_op jit(solution)/shard_map/all_gather | solution.py:158
  80.5 9.1 %all-gather.4 = bf16[8,96,3]{1,2,0:T(4,128)(2,1)S(1)} all-gather(bf16[1,96,3]{1,2,0:T(4,128)(2,1)S(1)} %bitcast.176), channel_id=1, replica_groups=mesh['o'=4,'c'=2,'s'=2,'h'=2] {'o','c'}, dimensions={0}, use_global_device_ids=true | all-gather | bytes 5184 | tf_op jit(solution)/shard_map/all_gather | solution.py:207
  91.3 12.7 %all_to_all.20 = bf16[4,2,49,768]{3,1,2,0:T(2,128)(2,1)S(1)} all-to-all(bf16[4,2,49,768]{3,1,2,0:T(2,128)(2,1)S(1)} %copy.90), channel_id=1, replica_groups=mesh['o'=4,'c'=2,'s'=2,'h'=2] {'c','h'}, dimensions={0} | all-to-all | bytes 1204224 | tf_op jit(solution)/shard_map/all_to_all | solution.py:172
  104.3 5.6 slice.47
  109.9 8.0 copy.128
  117.9 2.7 slice.49
  122.8 5.1 convert_bitcast_fusion.5.heads_ref
  127.9 8.6 %time_attend.1 = bf16[4,392,192]{2,1,0:T(8,128)(2,1)} custom-call(bf16[4,392,576]{2,1,0:T(8,128)(2,1)} %convert_bitcast_fusion.5.heads_ref), custom_call_target="tpu_custom_call" | custom-call | tf_op jit(solution)/shard_map/time_attend/pallas_call | solution.py:119
  139.8 3.5 all-to-all-start.1
  144.3 5.4 slice.50
  149.6 8.0 copy.130
  157.6 2.6 slice.52
  166.5 3.1 convert_bitcast_fusion.4.heads_ref
  169.6 7.9 space_attend.1
  177.5 2.3 fusion.39
  181.2 6.6 fusion.9
  187.8 3.9 all-gather.16.cloned.1.call-done
  191.7 18.3 %fusion.5 = bf16[4,392,768]{2,1,0:T(8,128)(2,1)S(1)} fusion(f32[392,4,768]{2,0,1:T(8,128)} %get-tuple-element.65, bf16[4,768,768]{2,1,0:T(8,128)(2,1)} %all-gather.16.cloned.1.call-done, f32[392,768]{1,0:T(8,128)S(1)} %copy-done.10, f32[]{:T(128)S(6)} %select_n.4), kind=kOutput, calls=%fused_computation.6 | convolution fusion | flops 1862332416 | bytes 13148164 | tf_op jit(solution)/shard_map/gn,tne->tge/dot_general | solution.py:219
  219.3 11.7 %space_attend_back.1 = bf16[4,392,576]{2,1,0:T(8,128)(2,1)} custom-call(bf16[4,392,576]{2,1,0:T(8,128)(2,1)} %convert_bitcast_fusion.4.heads_ref, bf16[4,392,192]{2,1,0:T(8,128)(2,1)} %bitcast.150), custom_call_target="tpu_custom_call" | custom-call | tf_op jit(solution)/shard_map/space_attend_back/pallas_call | solution.py:134
  231.0 4.2 convert_bitcast_fusion.2
  235.2 2.4 pad_maximum_fusion.1
  237.7 7.3 convert_bitcast_fusion.1
  245.1 6.9 convert_bitcast_fusion
  252.1 4.9 multiply_reduce_fusion.1
  261.6 27.6 %all_to_all.21 = bf16[4,2,49,768]{3,1,2,0:T(2,128)(2,1)S(1)} all-to-all(bf16[4,2,49,768]{3,1,2,0:T(2,128)(2,1)S(1)} %copy.103), channel_id=1, replica_groups=mesh['o'=4,'c'=2,'s'=2,'h'=2] {'c','h'}, dimensions={0} | all-to-all | bytes 1204224 | tf_op jit(solution)/shard_map/all_to_all | solution.py:172
  293.7 14.0 %time_attend_back.1 = bf16[4,392,576]{2,1,0:T(8,128)(2,1)} custom-call(bf16[4,392,576]{2,1,0:T(8,128)(2,1)} %convert_bitcast_fusion.5.heads_ref, bf16[4,392,192]{2,1,0:T(8,128)(2,1)} %bitcast.151), custom_call_target="tpu_custom_call" | custom-call | tf_op jit(solution)/shard_map/time_attend_back/pallas_call | solution.py:134
  312.0 2.5 pad_maximum_fusion
  314.5 5.0 fusion.15
  322.1 3.5 all-to-all-start.3
  325.7 9.5 %all-to-all-done.3 = bf16[4,2,49,768]{3,1,2,0:T(2,128)(2,1)S(1)} async-done(((bf16[4,2,49,768]{3,1,2,0:T(2,128)(2,1)}), bf16[4,2,49,768]{3,1,2,0:T(2,128)(2,1)S(1)}, u32[]{:S(2)}, u32[]{:S(2)}) %all-to-all-start.3) | async-done | bytes 602144 | tf_op jit(solution)/shard_map/all_to_all | solution.py:179
  336.8 2.7 reshape.155
  342.3 2.6 copy.120
  344.9 76.6 %reduce-scatter.24.cloned.1.call-done = bf16[1,768,768]{1,2,0:T(8,128)(2,1)} async-done(((bf16[4,768,768]{1,2,0:T(8,128)(2,1)}), bf16[1,768,768]{1,2,0:T(8,128)(2,1)}) %reduce-scatter.24.cloned.1.call-update) | async-done | bytes 1179664 | tf_op jit(solution)/shard_map/reduce_scatter | solution.py:164
  421.6 2.4 copy.122
  424.1 85.7 %reduce-scatter.26.cloned.1.call-done = bf16[1,768,768]{1,2,0:T(8,128)(2,1)} async-done(((bf16[4,768,768]{1,2,0:T(8,128)(2,1)}), bf16[1,768,768]{1,2,0:T(8,128)(2,1)}) %reduce-scatter.26.cloned.1.call-update) | async-done | bytes 1179664 | tf_op jit(solution)/shard_map/reduce_scatter | solution.py:164
  509.7 2.4 copy.124
  512.4 85.4 %reduce-scatter.20.cloned.1.call-done = bf16[1,768,768]{1,2,0:T(8,128)(2,1)} async-done(((bf16[4,768,768]{1,2,0:T(8,128)(2,1)}), bf16[1,768,768]{1,2,0:T(8,128)(2,1)}) %reduce-scatter.20.cloned.1.call-update) | async-done | bytes 1179664 | tf_op jit(solution)/shard_map/reduce_scatter | solution.py:164
  597.9 2.4 copy.118
  600.3 6.6 fusion.13
  609.5 25.9 %reduce-scatter.36.cloned.1.call-done = f32[96,3]{1,0:T(8,128)} async-done(((f32[768,3]{1,0:T(8,128)}), f32[96,3]{1,0:T(8,128)}) %reduce-scatter.36.cloned.1.call-update) | async-done | bytes 1168
  636.3 12.2 %psum.8 = f32[3,96]{1,0:T(4,128)} all-reduce(f32[3,96]{1,0:T(4,128)S(1)} %copy.127), channel_id=1, replica_groups=mesh['o'=4,'c'=2,'s'=2,'h'=2] {'s','h'}, use_global_device_ids=true, to_apply=%region_15.16 | all-reduce | flops 288 | bytes 2304 | tf_op jit(solution)/shard_map/psum | solution.py:269
  648.5 26.7 %reduce-scatter.30.cloned.1.call-done = bf16[96,768]{1,0:T(8,128)(2,1)} async-done(((bf16[768,768]{1,0:T(8,128)(2,1)}), bf16[96,768]{1,0:T(8,128)(2,1)}) %reduce-scatter.30.cloned.1.call-update) | async-done | bytes 147472
  677.2 37.9 %reduce-scatter.32.cloned.1.call-done = bf16[96,768]{1,0:T(8,128)(2,1)} async-done(((bf16[768,768]{1,0:T(8,128)(2,1)}), bf16[96,768]{1,0:T(8,128)(2,1)}) %reduce-scatter.32.cloned.1.call-update) | async-done | bytes 147472
  717.0 37.9 %reduce-scatter.34.cloned.1.call-done = bf16[96,768]{1,0:T(8,128)(2,1)} async-done(((bf16[768,768]{1,0:T(8,128)(2,1)}), bf16[96,768]{1,0:T(8,128)(2,1)}) %reduce-scatter.34.cloned.1.call-update) | async-done | bytes 147472
  757.5 37.3 %reduce-scatter.28.cloned.1.call-done = bf16[96,768]{1,0:T(8,128)(2,1)} async-done(((bf16[768,768]{1,0:T(8,128)(2,1)}), bf16[96,768]{1,0:T(8,128)(2,1)}) %reduce-scatter.28.cloned.1.call-update) | async-done | bytes 147472
  (168 shorter events, 63.4 us)
Async XLA Ops:
  7.2 97.1 %all-gather.10.cloned.1.call-start = ((), (), s32[]{:S(2)}) async-start(), calls=%async_computation.13 | async-start | bytes 5308416 | tf_op jit(solution)/shard_map/all_gather | solution.py:160
  9.3 19.8 %copy-start.19 = (bf16[3,96,192]{2,1,0:T(8,128)(2,1)S(1)}, bf16[3,96,192]{2,1,0:T(8,128)(2,1)}, u32[]{:S(2)}) copy-start(bf16[3,96,192]{2,1,0:T(8,128)(2,1)} %param.15) | copy-start | bytes 331780
  27.7 1.5 copy-start.22
  29.0 115.3 %all-gather.12.cloned.1.call-start = ((), (), s32[]{:S(2)}) async-start(), calls=%async_computation.14 | async-start | bytes 5308416 | tf_op jit(solution)/shard_map/all_gather | solution.py:160
  29.4 17.7 %copy-start.20 = (bf16[96,768]{1,0:T(8,128)(2,1)S(1)}, bf16[96,768]{1,0:T(8,128)(2,1)}, u32[]{:S(2)}) copy-start(bf16[96,768]{1,0:T(8,128)(2,1)} %param.17) | copy-start | bytes 442372
  47.0 17.7 %copy-start.21 = (bf16[768,96]{0,1:T(8,128)(2,1)S(1)}, bf16[768,96]{0,1:T(8,128)(2,1)}, u32[]{:S(2)}) copy-start(bf16[768,96]{0,1:T(8,128)(2,1)} %param.18) | copy-start | bytes 442372
  47.0 33.5 %copy-start.23 = (bf16[3,96]{1,0:T(4,128)(2,1)S(1)}, bf16[3,96]{1,0:T(4,128)(2,1)}, u32[]{:S(2)}) copy-start(bf16[3,96]{1,0:T(4,128)(2,1)} %param.12) | copy-start | bytes 1732
  47.0 42.7 %copy-start = (f32[392,768]{1,0:T(8,128)S(1)}, f32[392,768]{1,0:T(8,128)}, u32[]{:S(2)}) copy-start(f32[392,768]{1,0:T(8,128)} %param.10) | copy-start | bytes 3612676
  47.0 134.2 %all-gather.14.cloned.1.call-start = ((), (), s32[]{:S(2)}) async-start(), calls=%async_computation.15 | async-start | bytes 5308416 | tf_op jit(solution)/shard_map/all_gather | solution.py:160
  64.6 127.1 %all-gather.16.cloned.1.call-start = ((), (), s32[]{:S(2)}) async-start(), calls=%async_computation.16 | async-start | bytes 5308416 | tf_op jit(solution)/shard_map/all_gather | solution.py:160
  104.3 18.6 %copy-start.17 = (bf16[392,768,1]{1,0,2:T(8,128)(2,1)}, bf16[392,768,1]{1,0,2:T(8,128)(2,1)S(1)}, u32[]{:S(2)}) copy-start(bf16[392,768,1]{1,0,2:T(8,128)(2,1)S(1)} %reshape.163) | copy-start | bytes 1806340
  127.9 8.6 %copy-start.13 = (bf16[4,768,192]{1,2,0:T(8,128)(2,1)S(1)}, bf16[4,768,192]{1,2,0:T(8,128)(2,1)}, u32[]{:S(2)}) copy-start(bf16[4,768,192]{1,2,0:T(8,128)(2,1)} %copy.129) | copy-start | bytes 3538948
  139.8 22.6 %all-to-all-start.1 = ((bf16[4,2,49,768]{3,1,2,0:T(2,128)(2,1)}), bf16[4,2,49,768]{3,1,2,0:T(2,128)(2,1)S(1)}, u32[]{:S(2)}, u32[]{:S(2)}) async-start(bf16[4,2,49,768]{3,1,2,0:T(2,128)(2,1)} %copy.94), calls=%async_computation.1 | async-start | bytes 1204224 | tf_op jit(solution)/shard_map/all_to_all | solution.py:179
  143.3 199.0 %reduce-scatter.22.cloned.1.call-start = ((), (), s32[]{:S(2)}) async-start(), calls=%async_computation.18 | async-start | bytes 5898240 | tf_op jit(solution)/shard_map/reduce_scatter | solution.py:164
  164.1 2.4 copy-start.8
  165.8 11.8 %copy-start.1 = (f32[392,768]{1,0:T(8,128)}, f32[392,768]{1,0:T(8,128)S(1)}, u32[]{:S(2)}) copy-start(f32[392,768]{1,0:T(8,128)S(1)} %get-tuple-element.61) | copy-start | bytes 3612676
  179.9 1.0 copy-start.6
  181.2 10.5 %copy-start.10 = (f32[392,768]{1,0:T(8,128)S(1)}, f32[392,768]{1,0:T(8,128)}, u32[]{:S(2)}) copy-start(f32[392,768]{1,0:T(8,128)} %param.19) | copy-start | bytes 3612676
  191.7 18.3 %copy-start.7 = (f32[392,768]{1,0:T(8,128)S(1)}, f32[392,768]{1,0:T(8,128)}, u32[]{:S(2)}) copy-start(f32[392,768]{1,0:T(8,128)} %copy-done.6) | copy-start | bytes 3612676
  191.7 18.3 %copy-start.24 = (bf16[4,768,768]{2,1,0:T(8,128)(2,1)S(1)}, bf16[4,768,768]{2,1,0:T(8,128)(2,1)}, u32[]{:S(2)}) copy-start(bf16[4,768,768]{2,1,0:T(8,128)(2,1)} %all-gather.14.cloned.1.call-done) | copy-start | bytes 14155780
  210.1 2.3 copy-start.25
  212.4 1.3 copy-start.11
  213.7 1.3 copy-start.14
  215.0 1.1 copy-start.16
  231.0 4.2 copy-start.12
  237.6 183.9 %reduce-scatter.24.cloned.1.call-start = ((), (), s32[]{:S(2)}) async-start(), calls=%async_computation.19 | async-start | bytes 5898240 | tf_op jit(solution)/shard_map/reduce_scatter | solution.py:164
  245.0 264.7 %reduce-scatter.26.cloned.1.call-start = ((), (), s32[]{:S(2)}) async-start(), calls=%async_computation.20 | async-start | bytes 5898240 | tf_op jit(solution)/shard_map/reduce_scatter | solution.py:164
  252.1 345.8 %reduce-scatter.20.cloned.1.call-start = ((), (), s32[]{:S(2)}) async-start(), calls=%async_computation.17 | async-start | bytes 5898240 | tf_op jit(solution)/shard_map/reduce_scatter | solution.py:164
  252.1 5.0 copy-start.2
  257.6 1.0 copy-start.3
  293.7 14.0 %copy-start.15 = (bf16[4,392,192]{2,1,0:T(8,128)(2,1)S(1)}, bf16[4,392,192]{2,1,0:T(8,128)(2,1)}, u32[]{:S(2)}) copy-start(bf16[4,392,192]{2,1,0:T(8,128)(2,1)} %time_attend.1) | copy-start | bytes 1806340
  307.7 2.1 copy-start.9
  307.7 2.1 copy-start.18
  322.1 13.1 %all-to-all-start.3 = ((bf16[4,2,49,768]{3,1,2,0:T(2,128)(2,1)}), bf16[4,2,49,768]{3,1,2,0:T(2,128)(2,1)S(1)}, u32[]{:S(2)}, u32[]{:S(2)}) async-start(bf16[4,2,49,768]{3,1,2,0:T(2,128)(2,1)} %copy.106), calls=%async_computation.3 | async-start | bytes 1204224 | tf_op jit(solution)/shard_map/all_to_all | solution.py:179
  325.6 309.8 %reduce-scatter.36.cloned.1.call-start = ((), (), s32[]{:S(2)}) async-start(), calls=%async_computation.25 | async-start | bytes 442368
  342.2 332.9 %reduce-scatter.30.cloned.1.call-start = ((), (), s32[]{:S(2)}) async-start(), calls=%async_computation.22 | async-start | bytes 1327104
  344.9 370.2 %reduce-scatter.32.cloned.1.call-start = ((), (), s32[]{:S(2)}) async-start(), calls=%async_computation.23 | async-start | bytes 1327104
  424.0 330.9 %reduce-scatter.34.cloned.1.call-start = ((), (), s32[]{:S(2)}) async-start(), calls=%async_computation.24 | async-start | bytes 1327104
  512.1 282.7 %reduce-scatter.28.cloned.1.call-start = ((), (), s32[]{:S(2)}) async-start(), calls=%async_computation.21 | async-start | bytes 1327104
  600.3 6.6 copy-start.5
  606.9 1.3 copy-start.4
Sparse Core Ops, SparseCore 0:
  29.1 39.9 all-gather.9
  71.6 38.7 all-gather.11
  112.3 38.7 all-gather.13
  152.9 38.7 all-gather.15
  237.8 91.7 reduce-scatter.21
  331.7 89.8 reduce-scatter.23
  423.9 85.7 reduce-scatter.25
  512.0 85.7 reduce-scatter.19
  600.9 34.4 reduce-scatter.35
  638.5 36.6 reduce-scatter.29
  678.4 36.6 reduce-scatter.31
  718.2 36.6 reduce-scatter.33
  758.1 36.6 reduce-scatter.27
